TPU v7x, 256 devices: a whole 4x4x8 slice. The times are simulated.
256 devices in a mesh: comp: 32 (over z_lo, x, core), rows: 8 (over y, z_hi).
Axes of the slice: x: 4, y: 4, z: 8 (z_hi: 2, z_lo: 4; z = z_hi * 4 + z_lo), core: 2. Of those that a mesh axis runs over, the one named last changes fastest.
Arguments:
- hidden_states: bfloat16 [8, 2, 32, 128, 2560], P('rows', None, 'comp'), may hold values from -6 to 6
- queries: bfloat16 [8, 2, 32, 128, 1280], P('rows', None, 'comp'), may hold values from -900 to 900
- new_keys: bfloat16 [8, 2, 32, 128, 1280], P('rows', None, 'comp'), may hold values from -6 to 6
- new_values: bfloat16 [8, 2, 32, 128, 1280], P('rows', None, 'comp'), may hold values from -6 to 6
- out_grad: bfloat16 [8, 2, 32, 128, 1280], P('rows', None, 'comp'), may hold values from -6 to 6
- gate_weight: bfloat16 [2560, 128], replicated, may hold values from -0.125 to 0.125
- gate_bias: float32 [128], replicated, may hold values from -2 to 6
- prompt_state: float32 [8, 32, 2, 2, 2, 64, 640], P('rows', 'comp'), may hold values from -6 to 6
- owners: int32 [8, 2], P('rows'), may hold values from 0 to 31
- lengths: int32 [8, 2, 32], P('rows', None, 'comp'), may hold values from 32 to 128
- advantage: float32 [8, 2, 32], P('rows', None, 'comp'), may hold values from -4 to 4
Outputs:
- d_queries: bfloat16 [8, 2, 32, 128, 1280], P('rows', None, 'comp')
- d_keys: bfloat16 [8, 2, 32, 128, 1280], P('rows', None, 'comp')
- d_values: bfloat16 [8, 2, 32, 128, 1280], P('rows', None, 'comp')
- d_hidden: bfloat16 [8, 2, 32, 128, 2560], P('rows', None, 'comp')
- d_gate_weight: float32 [2560, 128], replicated
- d_gate_bias: float32 [128], replicated
- d_state: float32 [8, 2, 2, 2, 64, 640], P('rows', None, None, None, 'comp')
All inputs are finite; a program needn't handle non-finite values.
Results may differ from a plain program's by a relative error of at most 0.011.
Values sent between devices are 32-bit elements; how exact they have to be, the bound alone decides.
No kernel may reach another device: no remote copies, remote signals or barrier semaphores. Data moves between devices by JAX's collectives and lax.ppermute only.
A program may use at most 64 MiB of HBM per device.

v0:
```python
import jax
import jax.numpy as jnp
from jax import lax
from jax.sharding import PartitionSpec as P


def cut_along(value, dim, count):
    shape = value.shape
    blocks = value.reshape(*shape[:dim], count, shape[dim] // count, *shape[dim + 1 :])
    return jnp.moveaxis(blocks, dim, 0)


def sum_at_owner(value, axis, dim):
    count = lax.axis_size(axis)
    blocks = lax.all_to_all(cut_along(value, dim, count), axis, 0, 0, tiled=True)
    return jnp.sum(blocks, axis=0)


def slot_forward(gates, queries, keys_in, values_in, anchor_point):
    steps = queries.shape[0]
    heads = anchor_point.shape[1]
    slots = anchor_point.shape[2]
    width = anchor_point.shape[3]
    highest_score = lax.Precision.HIGHEST
    log_keep = jax.nn.log_sigmoid(gates).reshape(steps, heads, slots) / 8.0
    running = jnp.cumsum(log_keep, axis=0)
    inflow = -jnp.expm1(log_keep)
    places = jnp.arange(steps, dtype=jnp.int32)
    lower = (places[:, None] >= places[None, :])[:, :, None, None]
    between = running[:, None] - running[None, :]
    reach = jnp.where(lower, jnp.exp(jnp.where(lower, between, 0.0)), 0.0) * inflow[None]
    score_scale = width ** (-0.5)
    query_head_count = queries.astype(jnp.float32).reshape(steps, heads, width)
    key_heads = keys_in.astype(jnp.float32).reshape(steps, heads, width)
    value_heads = values_in.astype(jnp.float32).reshape(steps, heads, width)
    pairs = jnp.einsum("thd,jhd->thj", query_head_count, key_heads) * score_scale
    carried_state = jnp.exp(running)
    anchor_score_rows = (
        jnp.einsum("icv,crv->icr", query_head_count, anchor_point[0], precision=highest_score)
        * score_scale
    )
    scores = (
        jnp.einsum("tjhm,thj->thm", reach, pairs, precision=highest_score)
        + carried_state * anchor_score_rows
    )
    slot_probabilities = jax.nn.softmax(scores, axis=-1)
    mixing = jnp.einsum("thm,tjhm->thj", slot_probabilities, reach, precision=highest_score).astype(
        jnp.bfloat16
    )
    result_output = jnp.einsum("thj,jhd->thd", mixing.astype(jnp.float32), value_heads)
    result_output = result_output + jnp.einsum(
        "ivw,vwb->ivb", slot_probabilities * carried_state, anchor_point[1], precision=highest_score
    )
    return result_output.reshape(steps, heads * width)


def shards(
    hidden_states,
    queries,
    new_keys,
    new_values,
    out_grad,
    gate_weight,
    gate_bias,
    prompt_state,
    owners,
    lengths,
    advantage,
):
    local_states = prompt_state[0, 0]
    prompts = local_states.shape[0]
    steps = queries.shape[3]
    my_index = lax.axis_index("comp")
    owned = (owners[0] == my_index)[:, None, None, None, None]
    mine = jnp.where(owned, local_states, 0.0)
    pieces = sum_at_owner(mine, "comp", 3)
    anchors = lax.all_gather(pieces, "comp", axis=3, tiled=True)
    places = jnp.arange(steps, dtype=jnp.int32)
    sum_weight = jnp.zeros(gate_weight.shape, jnp.float32)
    sum_bias = jnp.zeros(gate_bias.shape, jnp.float32)
    state_terms = []
    out_q, out_k, out_v, out_x = ([], [], [], [])
    for prompt in range(prompts):
        list_q, list_k, list_v, list_x = ([], [], [], [])
        tokens = hidden_states[0, prompt, 0]
        gates = jnp.dot(tokens, gate_weight, preferred_element_type=jnp.float32) + gate_bias
        live = jnp.where(places < lengths[0, prompt, 0], 1.0, 0.0).astype(jnp.float32)
        cotangent = (advantage[0, prompt, 0] * live)[:, None] * out_grad[0, prompt, 0].astype(
            jnp.float32
        )
        result_output, pullback = jax.vjp(
            slot_forward,
            gates,
            queries[0, prompt, 0],
            new_keys[0, prompt, 0],
            new_values[0, prompt, 0],
            anchors[prompt],
        )
        grad_gates, grad_q, grad_k, grad_v, grad_anchor = pullback(cotangent)
        gates_low = grad_gates.astype(jnp.bfloat16)
        list_x.append(
            jnp.dot(gates_low, gate_weight.T, preferred_element_type=jnp.float32).astype(
                jnp.bfloat16
            )
        )
        sum_weight = sum_weight + jnp.dot(tokens.T, gates_low, preferred_element_type=jnp.float32)
        sum_bias = sum_bias + jnp.sum(grad_gates, axis=0)
        list_q.append(grad_q)
        list_k.append(grad_k)
        list_v.append(grad_v)
        state_terms.append(grad_anchor)
        out_q.append(jnp.stack(list_q))
        out_k.append(jnp.stack(list_k))
        out_v.append(jnp.stack(list_v))
        out_x.append(jnp.stack(list_x))
    state_grads = jnp.stack(state_terms)
    d_state = sum_at_owner(state_grads, "comp", 3)
    d_weight, d_bias = lax.psum((sum_weight, sum_bias), ("comp", "rows"))
    return (
        jnp.stack(out_q)[None],
        jnp.stack(out_k)[None],
        jnp.stack(out_v)[None],
        jnp.stack(out_x)[None],
        d_weight,
        d_bias,
        d_state[None],
    )


def solution(mesh):
    placed = (
        P("rows", None, "comp", None, None),
        P("rows", None, "comp", None, None),
        P("rows", None, "comp", None, None),
        P("rows", None, "comp", None, None),
        P("rows", None, "comp", None, None),
        P(),
        P(),
        P("rows", "comp", None, None, None, None, None),
        P("rows", None),
        P("rows", None, "comp"),
        P("rows", None, "comp"),
    )
    return jax.shard_map(
        shards,
        mesh=mesh,
        in_specs=placed,
        out_specs=(
            P("rows", None, "comp", None, None),
            P("rows", None, "comp", None, None),
            P("rows", None, "comp", None, None),
            P("rows", None, "comp", None, None),
            P(),
            P(),
            P("rows", None, None, None, "comp", None),
        ),
        check_vma=False,
    )
```

profile of v0, /device:TPU:2, one launch (start us, length us, event | category | flops | bytes accessed | tf_op | source)
XLA Modules:
  0.0 489.7 jit_solution(3050497754272828633)
XLA Ops:
  7.2 2.4 copy.282
  12.0 9.2 %all-to-all-start = ((f32[32,2,2,2,2,640]{5,4,3,2,1,0:T(2,128)}), f32[32,2,2,2,2,640]{5,4,3,2,1,0:T(2,128)S(1)}, u32[]{:S(2)}, u32[]{:S(2)}) async-start(f32[32,2,2,2,2,640]{5,4,3,2,1,0:T(2,128)} %copy.283), calls=%async_computation | async-start | bytes 2621440 | tf_op jit(solution)/shard_map/all_to_all | solution.py:15
  37.3 11.7 %multiply_reduce_fusion.3 = (f32[128,2,64]{2,1,0:T(2,128)}, f32[128,2,64]{2,1,0:T(2,128)S(1)}) fusion(f32[128,2,128]{2,1,0:T(2,128)} %copy.407, f32[128,2,64]{0,2,1:T(8,128)S(1)} %exponential-minus-one_negate_fusion.1, f32[128,2,64]{0,2,1:T(8,128)S(1)} %copy.280, f32[128,2,64]{2,1,0:T(2,128)S(1)} %copy-done.35, pred[128,128]{1,0:T(8,128)(4,1)S(1)} %iota_compare_fusion, ...), kind=kLoop, calls=%fused_computation.5 | loop fusion | flops 25133056 | bytes 802816
  62.7 8.5 %fusion.10 = f32[128,2,1,64]{3,2,1,0:T(1,128)S(1)} fusion(f32[128,2,64]{0,2,1:T(8,128)S(1)} %copy-done.56, f32[128,2,64]{0,2,1:T(8,128)S(1)} %copy.280, f32[128,2,64]{2,1,0:T(2,128)S(1)} %copy-done.36, pred[128,128]{1,0:T(8,128)(4,1)S(1)} %iota_compare_fusion, bf16[128,2,128,1]{2,0,1,3:T(8,128)(2,1)S(1)} %bitcast.433), kind=kOutput, calls=%fused_computation.19 | convolution fusion | flops 33554432 | bytes 344064 | tf_op jit(solution)/shard_map/transpose(jvp(thm,tjhm->thj))/dot_general | solution.py:47
  74.9 8.7 %fusion.4 = f32[128,2,1,64]{3,2,1,0:T(1,128)S(1)} fusion(f32[128,2,64]{0,2,1:T(8,128)S(1)} %copy-done.52, f32[128,2,64]{0,2,1:T(8,128)S(1)} %copy.300, f32[128,2,64]{2,1,0:T(2,128)S(1)} %copy-done.32, pred[128,128]{1,0:T(8,128)(4,1)S(1)} %iota_compare_fusion, bf16[128,2,128,1]{2,0,1,3:T(8,128)(2,1)S(1)} %bitcast.434), kind=kOutput, calls=%fused_computation.14 | convolution fusion | flops 33554432 | bytes 344064 | tf_op jit(solution)/shard_map/transpose(jvp(thm,tjhm->thj))/dot_general | solution.py:47
  83.7 30.7 %all-gather.2.cloned.1.call-done = f32[2,2,2,64,640]{4,2,1,0,3:T(2,128)} async-done(((f32[2,2,2,2,640]{4,2,1,0,3:T(2,128)}), f32[2,2,2,64,640]{4,2,1,0,3:T(2,128)}) %all-gather.2.cloned.1.call-update) | async-done | bytes 1310736 | tf_op jit(solution)/shard_map/all_gather | solution.py:77
  114.4 2.5 fusion.164
  130.3 2.3 convolution_bitcast_fusion.1
  138.9 11.8 %multiply_reduce_fusion.2 = (f32[128,2,128]{2,1,0:T(2,128)}, f32[128,2,128]{2,1,0:T(2,128)}) fusion(f32[128,2,64]{2,1,0:T(2,128)S(1)} %copy.408, f32[128,2,64]{0,2,1:T(8,128)} %copy-done.55, f32[128,2,64]{0,2,1:T(8,128)S(1)} %copy.280, f32[128,2,64]{2,1,0:T(2,128)} %fusion.171, pred[128,128]{1,0:T(8,128)(4,1)} %copy-done.59, f32[128,2,64]{0,2,1:T(8,128)} %copy-done.51, ...), kind=kLoop, calls=%fused_computation.4 | loop fusion | flops 25100288 | bytes 802816
  150.8 20.7 %fusion.13 = (f32[128,2,64]{0,2,1:T(8,128)}, f32[128,2,64]{2,1,0:T(2,128)}, f32[128,2,64]{0,2,1:T(8,128)}, f32[128,2,64]{0,2,1:T(8,128)}, f32[128,2,64]{2,1,0:T(2,128)}, /*index=5*/f32[128,2,64]{0,2,1:T(8,128)}) fusion(f32[128,2,64]{2,1,0:T(2,128)} %copy-done.44, f32[128,2,128]{2,1,0:T(2,128)S(1)} %copy-done.47, f32[128,2,64]{2,1,0:T(2,128)S(1)} %copy-done.42, ...), kind=kLoop, calls=%fused_computation.21 | loop fusion | flops 58621952 | bytes 1589248 | tf_op jit(solution)/shard_map/transpose(jvp())/reduce_sum | solution.py:30
  187.2 2.4 stack.25
  191.4 2.2 fusion.44
  204.4 5.9 %all-to-all-start.1 = ((f32[32,2,2,2,2,640]{5,4,3,2,1,0:T(2,128)}), f32[32,2,2,2,2,640]{5,4,3,2,1,0:T(2,128)S(1)}, u32[]{:S(2)}, u32[]{:S(2)}) async-start(f32[32,2,2,2,2,640]{5,4,3,2,1,0:T(2,128)} %copy_bitcast_fusion), calls=%async_computation.1 | async-start | bytes 2621440 | tf_op jit(solution)/shard_map/all_to_all | solution.py:15
  210.7 2.2 fusion.43
  214.8 2.9 fusion.36
  217.8 2.0 maximum_bitcast_fusion.2
  220.8 8.3 %fusion.8 = bf16[128,2,1,128]{3,2,1,0:T(2,128)(2,1)S(1)} fusion(f32[128,2,64,1]{2,3,1,0:T(1,128)S(1)} %copy-done.41, f32[128,2,64]{0,2,1:T(8,128)S(1)} %copy-done.58, f32[128,2,64]{0,2,1:T(8,128)S(1)} %copy.280, f32[128,2,64]{2,1,0:T(2,128)S(1)} %copy-done.38, pred[128,128]{1,0:T(8,128)(4,1)S(1)} %copy-done.61), kind=kOutput, calls=%fused_computation.18 | convolution fusion | flops 33554432 | bytes 344064 | tf_op jit(solution)/shard_map/jvp(thm,tjhm->thj)/dot_general | solution.py:47
  230.1 8.4 %fusion.2 = bf16[128,2,1,128]{3,2,1,0:T(2,128)(2,1)S(1)} fusion(f32[128,2,64,1]{2,3,1,0:T(1,128)S(1)} %copy-done.40, f32[128,2,64]{0,2,1:T(8,128)S(1)} %copy-done.54, f32[128,2,64]{0,2,1:T(8,128)S(1)} %copy.300, f32[128,2,64]{2,1,0:T(2,128)S(1)} %copy-done.34, pred[128,128]{1,0:T(8,128)(4,1)S(1)} %copy-done.61), kind=kOutput, calls=%fused_computation.13 | convolution fusion | flops 33554432 | bytes 344064 | tf_op jit(solution)/shard_map/jvp(thm,tjhm->thj)/dot_general | solution.py:47
  241.8 1.9 copy.321
  244.8 2.2 copy.340
  247.0 77.3 %psum.15 = f32[128]{0:T(128)} all-reduce(f32[128]{0:T(128)S(1)} %negate_add_fusion), channel_id=1, replica_groups=mesh['comp'=32,'rows'=8] {'comp','rows'}, use_global_device_ids=true, to_apply=%region_20.22 | all-reduce | flops 128 | bytes 1024 | tf_op jit(solution)/shard_map/psum | solution.py:118
  324.3 2.0 maximum_bitcast_fusion.3
  327.5 151.4 %all-reduce.6.cloned.1.call-done = f32[2560,128]{0,1:T(8,128)} async-done(((f32[2560,128]{0,1:T(8,128)}), f32[2560,128]{0,1:T(8,128)}) %all-reduce.6.cloned.1.call-update) | async-done | bytes 1310736 | tf_op jit(solution)/shard_map/psum | solution.py:118
  478.8 2.8 copy.343
  (255 shorter events, 94.3 us)
Async XLA Ops:
  7.2 14.6 %copy-start = (bf16[2560,128]{1,0:T(8,128)(2,1)S(1)}, bf16[2560,128]{1,0:T(8,128)(2,1)}, u32[]{:S(2)}) copy-start(bf16[2560,128]{1,0:T(8,128)(2,1)} %param.17) | copy-start | bytes 1966084
  12.0 42.2 %all-to-all-start = ((f32[32,2,2,2,2,640]{5,4,3,2,1,0:T(2,128)}), f32[32,2,2,2,2,640]{5,4,3,2,1,0:T(2,128)S(1)}, u32[]{:S(2)}, u32[]{:S(2)}) async-start(f32[32,2,2,2,2,640]{5,4,3,2,1,0:T(2,128)} %copy.283), calls=%async_computation | async-start | bytes 2621440 | tf_op jit(solution)/shard_map/all_to_all | solution.py:15
  21.2 93.2 %all-gather.2.cloned.1.call-start = ((), (), s32[]{:S(2)}) async-start(), calls=%async_computation.2 | async-start | bytes 1351680 | tf_op jit(solution)/shard_map/all_gather | solution.py:77
  24.1 13.2 %copy-start.31 = (f32[128,2,64]{2,1,0:T(2,128)}, f32[128,2,64]{2,1,0:T(2,128)S(1)}, u32[]{:S(2)}) copy-start(f32[128,2,64]{2,1,0:T(2,128)S(1)} %fusion.172) | copy-start | bytes 196612
  34.4 14.6 %copy-start.2 = (bf16[1,1,1,128,1280]{3,4,2,1,0:T(8,128)(2,1)}, bf16[1,1,1,128,1280]{3,4,2,1,0:T(8,128)(2,1)S(1)}, u32[]{:S(2)}) copy-start(bf16[1,1,1,128,1280]{3,4,2,1,0:T(8,128)(2,1)S(1)} %copy.399) | copy-start | bytes 983044
  35.5 39.4 %copy-start.59 = (pred[128,128]{1,0:T(8,128)(4,1)}, pred[128,128]{1,0:T(8,128)(4,1)S(1)}, u32[]{:S(2)}) copy-start(pred[128,128]{1,0:T(8,128)(4,1)S(1)} %iota_compare_fusion) | copy-start | bytes 49156
  36.4 12.6 %copy-start.51 = (f32[128,2,64]{0,2,1:T(8,128)}, f32[128,2,64]{0,2,1:T(8,128)S(1)}, u32[]{:S(2)}) copy-start(f32[128,2,64]{0,2,1:T(8,128)S(1)} %exponential-minus-one_negate_fusion) | copy-start | bytes 196612
  71.3 46.6 %copy-start.7 = (f32[128,2,1,64]{0,3,1,2:T(8,128)}, f32[128,2,1,64]{0,3,1,2:T(8,128)S(1)}, u32[]{:S(2)}) copy-start(f32[128,2,1,64]{0,3,1,2:T(8,128)S(1)} %copy.347) | copy-start | bytes 196612
  83.7 34.2 %copy-start.65 = (f32[128]{0:T(128)S(1)}, f32[128]{0:T(128)}, u32[]{:S(2)}) copy-start(f32[128]{0:T(128)} %copy-done.64) | copy-start | bytes 1540
  138.8 11.9 %copy-start.33 = (f32[128,2,64]{2,1,0:T(2,128)S(1)}, f32[128,2,64]{2,1,0:T(2,128)}, u32[]{:S(2)}) copy-start(f32[128,2,64]{2,1,0:T(2,128)} %copy-done.31) | copy-start | bytes 196612
  138.8 11.9 %copy-start.37 = (f32[128,2,64]{2,1,0:T(2,128)S(1)}, f32[128,2,64]{2,1,0:T(2,128)}, u32[]{:S(2)}) copy-start(f32[128,2,64]{2,1,0:T(2,128)} %fusion.171) | copy-start | bytes 196612
  138.8 11.9 %copy-start.42 = (f32[128,2,64]{2,1,0:T(2,128)S(1)}, f32[128,2,64]{2,1,0:T(2,128)}, u32[]{:S(2)}) copy-start(f32[128,2,64]{2,1,0:T(2,128)} %copy.323) | copy-start | bytes 196612
  138.8 11.9 %copy-start.43 = (f32[128,2,64]{2,1,0:T(2,128)S(1)}, f32[128,2,64]{2,1,0:T(2,128)}, u32[]{:S(2)}) copy-start(f32[128,2,64]{2,1,0:T(2,128)} %copy.330) | copy-start | bytes 196612
  138.8 11.9 %copy-start.46 = (f32[128,2,128]{2,1,0:T(2,128)S(1)}, f32[128,2,128]{2,1,0:T(2,128)}, u32[]{:S(2)}) copy-start(f32[128,2,128]{2,1,0:T(2,128)} %copy.409) | copy-start | bytes 393220
  138.8 11.9 %copy-start.47 = (f32[128,2,128]{2,1,0:T(2,128)S(1)}, f32[128,2,128]{2,1,0:T(2,128)}, u32[]{:S(2)}) copy-start(f32[128,2,128]{2,1,0:T(2,128)} %copy.407) | copy-start | bytes 393220
  138.8 11.9 %copy-start.48 = (f32[128,2,128]{2,1,0:T(2,128)S(1)}, f32[128,2,128]{2,1,0:T(2,128)}, u32[]{:S(2)}) copy-start(f32[128,2,128]{2,1,0:T(2,128)} %copy.322) | copy-start | bytes 393220
  138.8 11.9 %copy-start.49 = (f32[128,2,128]{2,1,0:T(2,128)S(1)}, f32[128,2,128]{2,1,0:T(2,128)}, u32[]{:S(2)}) copy-start(f32[128,2,128]{2,1,0:T(2,128)} %copy.329) | copy-start | bytes 393220
  150.7 21.7 %copy-start.8 = (f32[128,2,1,64]{0,3,1,2:T(8,128)S(1)}, f32[128,2,1,64]{0,3,1,2:T(8,128)}, u32[]{:S(2)}) copy-start(f32[128,2,1,64]{0,3,1,2:T(8,128)} %copy-done.7) | copy-start | bytes 196612
  150.7 21.7 %copy-start.10 = (f32[128,2,64]{0,2,1:T(8,128)S(1)}, f32[128,2,64]{0,2,1:T(8,128)}, u32[]{:S(2)}) copy-start(f32[128,2,64]{0,2,1:T(8,128)} %copy-done.9) | copy-start | bytes 196612
  150.7 21.7 %copy-start.21 = (f32[2,128,64]{1,2,0:T(8,128)S(1)}, f32[2,128,64]{1,2,0:T(8,128)}, u32[]{:S(2)}) copy-start(f32[2,128,64]{1,2,0:T(8,128)} %copy-done.20) | copy-start | bytes 196612
  150.8 21.7 %copy-start.27 = (f32[2,64,128]{2,1,0:T(8,128)S(1)}, f32[2,64,128]{2,1,0:T(8,128)}, u32[]{:S(2)}) copy-start(f32[2,64,128]{2,1,0:T(8,128)} %get-tuple-element.106) | copy-start | bytes 196612
  204.4 277.2 %all-to-all-start.1 = ((f32[32,2,2,2,2,640]{5,4,3,2,1,0:T(2,128)}), f32[32,2,2,2,2,640]{5,4,3,2,1,0:T(2,128)S(1)}, u32[]{:S(2)}, u32[]{:S(2)}) async-start(f32[32,2,2,2,2,640]{5,4,3,2,1,0:T(2,128)} %copy_bitcast_fusion), calls=%async_computation.1 | async-start | bytes 2621440 | tf_op jit(solution)/shard_map/all_to_all | solution.py:15
  210.3 268.6 %all-reduce.6.cloned.1.call-start = ((), (), s32[]{:S(2)}) async-start(), calls=%async_computation.3 | async-start | bytes 2621440 | tf_op jit(solution)/shard_map/psum | solution.py:118
  244.8 81.5 %copy-start.4 = (bf16[1,1,128,2560]{3,2,1,0:T(8,128)(2,1)S(1)}, bf16[1,1,128,2560]{3,2,1,0:T(8,128)(2,1)}, u32[]{:S(2)}) copy-start(bf16[1,1,128,2560]{3,2,1,0:T(8,128)(2,1)} %fusion.37) | copy-start | bytes 1966084
  (52 other events, 276.8 us)
Sparse Core Ops, SparseCore 0:
  55.4 58.9 all-gather.1
  217.9 260.9 all-reduce.5
where the time goes:
time: 494 us; the launch traced here: 490 us
  waiting for transfers between devices  182 us (37%)
  blocking collectives  77.3 us (16%)
  other arithmetic  76.5 us (15%)
  matrix products  65.9 us (13%)
  local copies, waits for them, and re-layouts  56.7 us (11%)
  starting transfers between devices  16.1 us (3%)
  between operations  15.1 us (3%)
    psum x1, waiting for transfers between devices, shards(): d_weight, d_bias = lax.psum((sum_weight, sum_bias), ('comp', 'rows'))  151 us
    psum x1, blocking collectives, shards(): d_weight, d_bias = lax.psum((sum_weight, sum_bias), ('comp', 'rows'))  77.3 us
    dot_general x4, matrix products, slot_forward(): jnp.einsum('thm,tjhm->thj', slot_probabilities, reach, precision=highest_...  33.9 us
    all_gather x1, waiting for transfers between devices, shards(): anchors = lax.all_gather(pieces, 'comp', axis=3, tiled=True)  30.7 us
    unnamed x3, other arithmetic  24.6 us
    reduce_sum x1, other arithmetic, slot_forward(): between = running[:, None] - running[None, :]  20.7 us
    unnamed x158, local copies, waits for them, and re-layouts  18 us
    all_to_all x2, starting transfers between devices, sum_at_owner(): lax.all_to_all(cut_along(value, dim, count), axis, 0, 0, tiled=True)  15.1 us
  transfers between devices with their start and end apart: 4, of which 2 were waited for; matrix products, arithmetic and copies ran while one was open for 21% of the time, Pallas kernels for 0%

commit v1 on v0

--- a/solution.py
+++ b/solution.py
@@ -2,6 +2,11 @@
 import jax.numpy as jnp
 from jax import lax
 from jax.sharding import PartitionSpec as P
+
+
+def one_after_other(value_2, axis_one, axis_two):
+    partial = lax.psum(value_2, axis_one)
+    return lax.psum(partial, axis_two)
 
 
 def cut_along(value, dim, count):
@@ -115,7 +120,7 @@
         out_x.append(jnp.stack(list_x))
     state_grads = jnp.stack(state_terms)
     d_state = sum_at_owner(state_grads, "comp", 3)
-    d_weight, d_bias = lax.psum((sum_weight, sum_bias), ("comp", "rows"))
+    d_weight, d_bias = one_after_other((sum_weight, sum_bias), "rows", "comp")
     return (
         jnp.stack(out_q)[None],
         jnp.stack(out_k)[None],

time: 494 us -> 669 us (1.35)
  the two profiles are of different devices: /device:TPU:2 before, /device:TPU:1 now
where the time goes in v1:
time: 669 us; the launch traced here: 662 us
  waiting for transfers between devices  349 us (52%)
  blocking collectives  97.8 us (15%)
  other arithmetic  71 us (11%)
  matrix products  64.9 us (10%)
  local copies, waits for them, and re-layouts  48.6 us (7%)
  starting transfers between devices  15.7 us (2%)
  between operations  15 us (2%)
    psum x1, waiting for transfers between devices, one_after_other(): return lax.psum(partial, axis_two)  179 us
    psum x1, waiting for transfers between devices, one_after_other(): partial = lax.psum(value_2, axis_one)  139 us
    psum x1, blocking collectives, one_after_other(): return lax.psum(partial, axis_two)  74.9 us
    dot_general x4, matrix products, slot_forward(): jnp.einsum('thm,tjhm->thj', slot_probabilities, reach, precision=highest_...  36.4 us
    all_gather x1, waiting for transfers between devices, shards(): anchors = lax.all_gather(pieces, 'comp', axis=3, tiled=True)  31.3 us
    unnamed x3, other arithmetic  23.6 us
    psum x1, blocking collectives, one_after_other(): partial = lax.psum(value_2, axis_one)  22.9 us
    reduce_sum x1, other arithmetic, slot_forward(): between = running[:, None] - running[None, :]  19.5 us
  transfers between devices with their start and end apart: 5, of which 3 were waited for; matrix products, arithmetic and copies ran while one was open for 12% of the time, Pallas kernels for 0%

profile of v1, /device:TPU:1, one launch (start us, length us, event | category | flops | bytes accessed | tf_op | source)
XLA Modules:
  0.0 661.8 jit_solution(1098314084651012816)
XLA Ops:
  7.2 2.4 copy.282
  12.0 10.1 %all-to-all-start = ((f32[32,2,2,2,2,640]{5,4,3,2,1,0:T(2,128)}), f32[32,2,2,2,2,640]{5,4,3,2,1,0:T(2,128)S(1)}, u32[]{:S(2)}, u32[]{:S(2)}) async-start(f32[32,2,2,2,2,640]{5,4,3,2,1,0:T(2,128)} %copy.283), calls=%async_computation | async-start | bytes 2621440 | tf_op jit(solution)/shard_map/all_to_all | solution.py:20
  22.2 2.2 negate_multiply_fusion
  37.0 11.7 %multiply_reduce_fusion.3 = (f32[128,2,64]{2,1,0:T(2,128)}, f32[128,2,64]{2,1,0:T(2,128)S(1)}) fusion(f32[128,2,128]{2,1,0:T(2,128)} %copy.407, f32[128,2,64]{0,2,1:T(8,128)S(1)} %exponential-minus-one_negate_fusion.1, f32[128,2,64]{0,2,1:T(8,128)S(1)} %copy.280, f32[128,2,64]{2,1,0:T(2,128)S(1)} %copy-done.38, pred[128,128]{1,0:T(8,128)(4,1)S(1)} %iota_compare_fusion, ...), kind=kLoop, calls=%fused_computation.5 | loop fusion | flops 25133056 | bytes 802816
  62.5 8.5 %fusion.10 = f32[128,2,1,64]{3,2,1,0:T(1,128)S(1)} fusion(f32[128,2,64]{0,2,1:T(8,128)S(1)} %copy-done.63, f32[128,2,64]{0,2,1:T(8,128)S(1)} %copy.280, f32[128,2,64]{2,1,0:T(2,128)S(1)} %copy-done.39, pred[128,128]{1,0:T(8,128)(4,1)S(1)} %iota_compare_fusion, bf16[128,2,128,1]{2,0,1,3:T(8,128)(2,1)S(1)} %bitcast.433), kind=kOutput, calls=%fused_computation.19 | convolution fusion | flops 33554432 | bytes 344064 | tf_op jit(solution)/shard_map/transpose(jvp(thm,tjhm->thj))/dot_general | solution.py:52
  74.8 8.5 %fusion.4 = f32[128,2,1,64]{3,2,1,0:T(1,128)S(1)} fusion(f32[128,2,64]{0,2,1:T(8,128)S(1)} %copy-done.58, f32[128,2,64]{0,2,1:T(8,128)S(1)} %copy.300, f32[128,2,64]{2,1,0:T(2,128)S(1)} %copy-done.33, pred[128,128]{1,0:T(8,128)(4,1)S(1)} %iota_compare_fusion, bf16[128,2,128,1]{2,0,1,3:T(8,128)(2,1)S(1)} %bitcast.434), kind=kOutput, calls=%fused_computation.14 | convolution fusion | flops 33554432 | bytes 344064 | tf_op jit(solution)/shard_map/transpose(jvp(thm,tjhm->thj))/dot_general | solution.py:52
  83.4 31.3 %all-gather.2.cloned.1.call-done = f32[2,2,2,64,640]{4,2,1,0,3:T(2,128)} async-done(((f32[2,2,2,2,640]{4,2,1,0,3:T(2,128)}), f32[2,2,2,64,640]{4,2,1,0,3:T(2,128)}) %all-gather.2.cloned.1.call-update) | async-done | bytes 1310736 | tf_op jit(solution)/shard_map/all_gather | solution.py:82
  114.7 2.5 fusion.164
  134.7 9.7 %fusion.8 = bf16[128,2,1,128]{3,2,1,0:T(2,128)(2,1)S(1)} fusion(f32[128,2,64,1]{2,3,1,0:T(1,128)} %copy.388, f32[128,2,64]{0,2,1:T(8,128)} %copy-done.62, f32[128,2,64]{0,2,1:T(8,128)S(1)} %copy.280, f32[128,2,64]{2,1,0:T(2,128)} %copy-done.37, pred[128,128]{1,0:T(8,128)(4,1)} %copy-done.66), kind=kOutput, calls=%fused_computation.18 | convolution fusion | flops 33554432 | bytes 344064 | tf_op jit(solution)/shard_map/jvp(thm,tjhm->thj)/dot_general | solution.py:52
  148.7 9.7 %fusion.2 = bf16[128,2,1,128]{3,2,1,0:T(2,128)(2,1)} fusion(f32[128,2,64,1]{2,3,1,0:T(1,128)S(1)} %copy.390, f32[128,2,64]{0,2,1:T(8,128)S(1)} %copy-done.59, f32[128,2,64]{0,2,1:T(8,128)S(1)} %copy.300, f32[128,2,64]{2,1,0:T(2,128)S(1)} %copy-done.34, pred[128,128]{1,0:T(8,128)(4,1)} %copy-done.66), kind=kOutput, calls=%fused_computation.13 | convolution fusion | flops 33554432 | bytes 344064 | tf_op jit(solution)/shard_map/jvp(thm,tjhm->thj)/dot_general | solution.py:52
  158.5 10.7 %multiply_reduce_fusion.2 = (f32[128,2,128]{2,1,0:T(2,128)}, f32[128,2,128]{2,1,0:T(2,128)}) fusion(f32[128,2,64]{2,1,0:T(2,128)S(1)} %copy-done.48, f32[128,2,64]{0,2,1:T(8,128)S(1)} %copy-done.64, f32[128,2,64]{0,2,1:T(8,128)S(1)} %copy.280, f32[128,2,64]{2,1,0:T(2,128)S(1)} %copy-done.40, pred[128,128]{1,0:T(8,128)(4,1)S(1)} %copy-done.67, ...), kind=kLoop, calls=%fused_computation.4 | loop fusion | flops 25100288 | bytes 802816
  171.0 2.1 fusion.41
  173.0 2.2 fusion.44
  175.4 19.5 %fusion.13 = (f32[128,2,64]{0,2,1:T(8,128)}, f32[128,2,64]{2,1,0:T(2,128)S(1)}, f32[128,2,64]{0,2,1:T(8,128)}, f32[128,2,64]{0,2,1:T(8,128)}, f32[128,2,64]{2,1,0:T(2,128)}, /*index=5*/f32[128,2,64]{0,2,1:T(8,128)}) fusion(f32[128,2,64]{2,1,0:T(2,128)S(1)} %copy-done.49, f32[128,2,128]{2,1,0:T(2,128)S(1)} %copy-done.53, f32[128,2,64]{2,1,0:T(2,128)S(1)} %copy-done.46, ...), kind=kLoop, calls=%fused_computation.21 | loop fusion | flops 58621952 | bytes 1589248 | tf_op jit(solution)/shard_map/transpose(jvp())/reduce_sum | solution.py:35
  213.8 1.9 copy.320
  215.8 1.9 copy.317
  218.7 5.3 all-to-all-start.1
  224.0 1.9 convolution_convert_fusion.4
  225.9 1.9 copy.321
  231.7 138.5 %all-reduce.7.cloned.1.call-done = f32[2560,128]{0,1:T(8,128)} async-done(((f32[2560,128]{0,1:T(8,128)}), f32[2560,128]{0,1:T(8,128)}) %all-reduce.7.cloned.1.call-update) | async-done | bytes 1310736 | tf_op jit(solution)/shard_map/psum | solution.py:8
  371.4 22.9 %psum.30 = f32[128]{0:T(128)S(1)} all-reduce(f32[128]{0:T(128)S(1)} %negate_add_fusion), channel_id=1, replica_groups=mesh['comp'=32,'rows'=8] {'rows'}, use_global_device_ids=true, to_apply=%region_21.23 | all-reduce | flops 128 | bytes 1024 | tf_op jit(solution)/shard_map/psum | solution.py:8
  394.3 74.9 %psum.31 = f32[128]{0:T(128)} all-reduce(f32[128]{0:T(128)S(1)} %psum.30), channel_id=1, replica_groups=mesh['comp'=32,'rows'=8] {'comp'}, use_global_device_ids=true, to_apply=%region_22.24 | all-reduce | flops 128 | bytes 1024 | tf_op jit(solution)/shard_map/psum | solution.py:9
  473.4 179.0 %all-reduce.9.cloned.1.call-done = f32[2560,128]{0,1:T(8,128)} async-done(((f32[2560,128]{0,1:T(8,128)}), f32[2560,128]{0,1:T(8,128)}) %all-reduce.9.cloned.1.call-update) | async-done | bytes 1310736 | tf_op jit(solution)/shard_map/psum | solution.py:9
  652.3 2.8 copy.343
  (275 shorter events, 84.9 us)
Async XLA Ops:
  7.2 15.0 %copy-start = (bf16[2560,128]{1,0:T(8,128)(2,1)S(1)}, bf16[2560,128]{1,0:T(8,128)(2,1)}, u32[]{:S(2)}) copy-start(bf16[2560,128]{1,0:T(8,128)(2,1)} %param.17) | copy-start | bytes 1966084
  12.0 41.9 %all-to-all-start = ((f32[32,2,2,2,2,640]{5,4,3,2,1,0:T(2,128)}), f32[32,2,2,2,2,640]{5,4,3,2,1,0:T(2,128)S(1)}, u32[]{:S(2)}, u32[]{:S(2)}) async-start(f32[32,2,2,2,2,640]{5,4,3,2,1,0:T(2,128)} %copy.283), calls=%async_computation | async-start | bytes 2621440 | tf_op jit(solution)/shard_map/all_to_all | solution.py:20
  22.2 92.6 %all-gather.2.cloned.1.call-start = ((), (), s32[]{:S(2)}) async-start(), calls=%async_computation.2 | async-start | bytes 1351680 | tf_op jit(solution)/shard_map/all_gather | solution.py:82
  25.7 11.2 %copy-start.32 = (f32[128,2,64]{2,1,0:T(2,128)}, f32[128,2,64]{2,1,0:T(2,128)S(1)}, u32[]{:S(2)}) copy-start(f32[128,2,64]{2,1,0:T(2,128)S(1)} %fusion.172) | copy-start | bytes 196612
  34.1 14.6 %copy-start.3 = (bf16[1,1,1,128,1280]{3,4,2,1,0:T(8,128)(2,1)}, bf16[1,1,1,128,1280]{3,4,2,1,0:T(8,128)(2,1)S(1)}, u32[]{:S(2)}) copy-start(bf16[1,1,1,128,1280]{3,4,2,1,0:T(8,128)(2,1)S(1)} %copy.399) | copy-start | bytes 983044
  35.2 39.6 %copy-start.66 = (pred[128,128]{1,0:T(8,128)(4,1)}, pred[128,128]{1,0:T(8,128)(4,1)S(1)}, u32[]{:S(2)}) copy-start(pred[128,128]{1,0:T(8,128)(4,1)S(1)} %iota_compare_fusion) | copy-start | bytes 49156
  36.0 12.6 %copy-start.57 = (f32[128,2,64]{0,2,1:T(8,128)}, f32[128,2,64]{0,2,1:T(8,128)S(1)}, u32[]{:S(2)}) copy-start(f32[128,2,64]{0,2,1:T(8,128)S(1)} %exponential-minus-one_negate_fusion) | copy-start | bytes 196612
  37.0 11.7 %copy-start.62 = (f32[128,2,64]{0,2,1:T(8,128)}, f32[128,2,64]{0,2,1:T(8,128)S(1)}, u32[]{:S(2)}) copy-start(f32[128,2,64]{0,2,1:T(8,128)S(1)} %exponential-minus-one_negate_fusion.1) | copy-start | bytes 196612
  55.0 315.2 %all-reduce.7.cloned.1.call-start = ((), (), s32[]{:S(2)}) async-start(), calls=%async_computation.3 | async-start | bytes 2621440 | tf_op jit(solution)/shard_map/psum | solution.py:8
  71.1 47.1 %copy-start.7 = (f32[128,2,1,64]{0,3,1,2:T(8,128)}, f32[128,2,1,64]{0,3,1,2:T(8,128)S(1)}, u32[]{:S(2)}) copy-start(f32[128,2,1,64]{0,3,1,2:T(8,128)S(1)} %copy.347) | copy-start | bytes 196612
  72.7 10.6 %copy-start.71 = (f32[128]{0:T(128)}, f32[128]{0:T(128)S(1)}, u32[]{:S(2)}) copy-start(f32[128]{0:T(128)S(1)} %fusion.147) | copy-start | bytes 1540
  83.3 44.7 %copy-start.5 = (f32[128,2,1,64]{0,3,1,2:T(8,128)}, f32[128,2,1,64]{0,3,1,2:T(8,128)S(1)}, u32[]{:S(2)}) copy-start(f32[128,2,1,64]{0,3,1,2:T(8,128)S(1)} %copy.368) | copy-start | bytes 196612
  83.4 34.8 %copy-start.76 = (f32[128]{0:T(128)S(1)}, f32[128]{0:T(128)}, u32[]{:S(2)}) copy-start(f32[128]{0:T(128)} %copy-done.75) | copy-start | bytes 1540
  134.7 10.6 %copy-start.18 = (f32[1,2,64,640]{3,2,1,0:T(8,128)S(1)}, f32[1,2,64,640]{3,2,1,0:T(8,128)}, u32[]{:S(2)}) copy-start(f32[1,2,64,640]{3,2,1,0:T(8,128)} %convolution_bitcast_fusion.2) | copy-start | bytes 983044
  134.7 10.6 %copy-start.21 = (f32[1,2,64,640]{3,2,1,0:T(8,128)S(1)}, f32[1,2,64,640]{3,2,1,0:T(8,128)}, u32[]{:S(2)}) copy-start(f32[1,2,64,640]{3,2,1,0:T(8,128)} %convolution_bitcast_fusion.3) | copy-start | bytes 983044
  158.5 14.5 %copy-start.4 = (bf16[1,1,1,128,1280]{3,4,2,1,0:T(8,128)(2,1)S(1)}, bf16[1,1,1,128,1280]{3,4,2,1,0:T(8,128)(2,1)}, u32[]{:S(2)}) copy-start(bf16[1,1,1,128,1280]{3,4,2,1,0:T(8,128)(2,1)} %copy-done.3) | copy-start | bytes 983044
  175.3 19.7 %copy-start.8 = (f32[128,2,1,64]{0,3,1,2:T(8,128)S(1)}, f32[128,2,1,64]{0,3,1,2:T(8,128)}, u32[]{:S(2)}) copy-start(f32[128,2,1,64]{0,3,1,2:T(8,128)} %copy-done.7) | copy-start | bytes 196612
  175.3 19.7 %copy-start.10 = (f32[128,2,64]{0,2,1:T(8,128)S(1)}, f32[128,2,64]{0,2,1:T(8,128)}, u32[]{:S(2)}) copy-start(f32[128,2,64]{0,2,1:T(8,128)} %copy-done.9) | copy-start | bytes 196612
  175.3 19.7 %copy-start.26 = (f32[2,128,64]{1,2,0:T(8,128)S(1)}, f32[2,128,64]{1,2,0:T(8,128)}, u32[]{:S(2)}) copy-start(f32[2,128,64]{1,2,0:T(8,128)} %copy-done.25) | copy-start | bytes 196612
  175.4 19.7 %copy-start.29 = (f32[2,64,128]{2,1,0:T(8,128)S(1)}, f32[2,64,128]{2,1,0:T(8,128)}, u32[]{:S(2)}) copy-start(f32[2,64,128]{2,1,0:T(8,128)} %get-tuple-element.106) | copy-start | bytes 196612
  218.7 253.7 %all-to-all-start.1 = ((f32[32,2,2,2,2,640]{5,4,3,2,1,0:T(2,128)}), f32[32,2,2,2,2,640]{5,4,3,2,1,0:T(2,128)S(1)}, u32[]{:S(2)}, u32[]{:S(2)}) async-start(f32[32,2,2,2,2,640]{5,4,3,2,1,0:T(2,128)} %copy_bitcast_fusion), calls=%async_computation.1 | async-start | bytes 2621440 | tf_op jit(solution)/shard_map/all_to_all | solution.py:20
  224.0 428.4 %all-reduce.9.cloned.1.call-start = ((), (), s32[]{:S(2)}) async-start(), calls=%async_computation.4 | async-start | bytes 2621440 | tf_op jit(solution)/shard_map/psum | solution.py:9
  231.5 138.8 %copy-start.17 = (bf16[128,2,640]{0,2,1:T(8,128)(2,1)S(1)}, bf16[128,2,640]{0,2,1:T(8,128)(2,1)}, u32[]{:S(2)}) copy-start(bf16[128,2,640]{0,2,1:T(8,128)(2,1)} %copy.298) | copy-start | bytes 983044
  370.3 99.0 %copy-start.31 = (f32[128,128]{0,1:T(8,128)S(1)}, f32[128,128]{0,1:T(8,128)}, u32[]{:S(2)}) copy-start(f32[128,128]{0,1:T(8,128)} %copy-done.30) | copy-start | bytes 196612
  (61 other events, 299.1 us)
Sparse Core Ops, SparseCore 0:
  55.1 59.5 all-gather.1
  212.2 157.9 all-reduce.6
  372.8 279.4 all-reduce.8
